TPU v7x, 32 devices: a whole 2x2x4 slice. The times are simulated.
32 devices in a mesh: head: 8 (over z, y), ctx: 4 (over x, core).
Axes of the slice: x: 2, y: 2, z: 4, core: 2. Of those that a mesh axis runs over, the one named last changes fastest.
Arguments:
- query: bfloat16 [3072, 4096], P(('ctx', 'head')), may hold values from -8 to 8
- key: bfloat16 [3072, 2048], P(('ctx', 'head')), may hold values from -8 to 8
- value: bfloat16 [3072, 2048], P(('ctx', 'head')), may hold values from -8 to 8
- block_order: int32 [8], replicated, may hold values from 0 to 7, each once
Outputs:
- attended: bfloat16 [3072, 4096], P('ctx', 'head')
Inputs may be any that keep to these rules, and one draw needn't show every extreme that they name: `block_order`: each storage block index 0 to 7 appears exactly once.
All inputs are finite; a program needn't handle non-finite values.
Results may differ from a plain program's by a relative error of at most 0.0049.
Values may be sent and summed in bfloat16 or wider, within the bound.
A program may use at most 128 MiB of HBM per device.

v0:
```python
import jax
import jax.numpy as jnp
from jax import lax
from jax.sharding import PartitionSpec as P

HEAD_WIDTH = 128
query_scale = 1.0 / 12.0
softcap_limit = 50.0


def from_behind(value, axis, by):
    size = lax.axis_size(axis)
    return lax.ppermute(value, axis, [(i, (i + by) % size) for i in range(size)])


def block_pos(block_order, which_block, block_len):
    first = lax.dynamic_index_in_dim(block_order, which_block, 0, keepdims=False)
    return first * block_len + lax.iota(jnp.int32, block_len)


def add_block(totals, query_rows, query_pos, key_block, value_block, key_pos):
    numerator, denominator = totals
    scores = (
        jnp.einsum("rhgd,khd->hgrk", query_rows, key_block, preferred_element_type=jnp.float32)
        * query_scale
    )
    capped = softcap_limit * jnp.tanh(scores / softcap_limit)
    visible = key_pos[None, :] <= query_pos[:, None]
    weights = jnp.where(visible[None, None], jnp.exp(capped), jnp.zeros_like(capped))
    denominator = denominator + jnp.sum(weights, axis=-1)
    numerator = numerator + jnp.einsum(
        "hgrk,khd->rhgd",
        weights.astype(jnp.bfloat16),
        value_block,
        preferred_element_type=jnp.float32,
    )
    return (numerator, denominator)


def shards(query, key, value, block_order):
    query, key, value = (
        lax.all_to_all(query, "head", split_axis=1, concat_axis=0, tiled=True),
        lax.all_to_all(key, "head", split_axis=1, concat_axis=0, tiled=True),
        lax.all_to_all(value, "head", split_axis=1, concat_axis=0, tiled=True),
    )
    row_count = query.shape[0]
    block_len = row_count // 2
    kv_heads = key.shape[1] // HEAD_WIDTH
    group_size = query.shape[1] // key.shape[1]
    query_rows = query.reshape(row_count, kv_heads, group_size, HEAD_WIDTH)
    kv_pair = jnp.stack(
        [
            key.reshape(row_count, kv_heads, HEAD_WIDTH),
            value.reshape(row_count, kv_heads, HEAD_WIDTH),
        ]
    )
    cycle_size = lax.axis_size("ctx")
    cycle_index = lax.axis_index("ctx")
    query_pos = jnp.concatenate(
        [
            block_pos(block_order, 2 * cycle_index, block_len),
            block_pos(block_order, 2 * cycle_index + 1, block_len),
        ]
    )
    start_totals = (
        jnp.zeros((row_count, kv_heads, group_size, HEAD_WIDTH), jnp.float32),
        jnp.zeros((kv_heads, group_size, row_count), jnp.float32),
    )

    def add_shard(totals, held, source):
        for which_half in range(2):
            lower = which_half * block_len
            key_pos = block_pos(block_order, 2 * source + which_half, block_len)
            totals = add_block(
                totals,
                query_rows,
                query_pos,
                held[0, lower : lower + block_len],
                held[1, lower : lower + block_len],
                key_pos,
            )
        return totals

    totals = add_shard(start_totals, kv_pair, cycle_index)

    def from_lower(held):
        return from_behind(held, "ctx", 1)

    def turn_both(turn_index, state):
        forward_kv, backward_kv, sums = state
        forward_kv = from_lower(forward_kv)
        backward_kv = from_behind(backward_kv, "ctx", -1)
        sums = add_shard(sums, forward_kv, (cycle_index - turn_index) % cycle_size)
        sums = add_shard(sums, backward_kv, (cycle_index + turn_index) % cycle_size)
        return (forward_kv, backward_kv, sums)

    forward_kv, backward_kv, totals = lax.fori_loop(
        1, cycle_size // 2, turn_both, (kv_pair, kv_pair, totals)
    )
    forward_kv = from_lower(forward_kv)
    totals = add_shard(totals, forward_kv, (cycle_index + cycle_size // 2) % cycle_size)
    numerator, denominator = totals
    result = numerator / jnp.transpose(denominator, (2, 0, 1))[..., None]
    return result.reshape(row_count, kv_heads * group_size * HEAD_WIDTH).astype(jnp.bfloat16)


def solution(mesh):
    placed = (P(("ctx", "head"), None), P(("ctx", "head"), None), P(("ctx", "head"), None), P())
    return jax.shard_map(
        shards, mesh=mesh, in_specs=placed, out_specs=P("ctx", "head"), check_vma=False
    )
```

profile of v0, /device:TPU:1, one launch (start us, length us, event | category | flops | bytes accessed | tf_op | source)
XLA Modules:
  0.0 99.2 jit_solution(4919566508490505928)
XLA Ops:
  0.0 1.8 %copy.134 = bf16[12,8,8,256]{3,2,0,1:T(8,128)(2,1)} copy(bf16[12,8,8,256]{3,2,1,0:T(8,128)(2,1)} %bitcast.235) | data formatting | bytes 786432 | tf_op jit(solution)/shard_map/all_to_all | solution.py:43
  1.8 6.4 %all-to-all-start = ((bf16[96,8,256]{2,0,1:T(8,128)(2,1)}), bf16[96,8,256]{2,0,1:T(8,128)(2,1)S(1)}, u32[]{:S(2)}, u32[]{:S(2)}) async-start(bf16[96,8,256]{2,0,1:T(8,128)(2,1)} %bitcast.228), calls=%async_computation | async-start | bytes 786432 | tf_op jit(solution)/shard_map/all_to_all | solution.py:43
  8.1 1.8 %copy.135 = bf16[12,8,8,256]{3,2,0,1:T(8,128)(2,1)} copy(bf16[12,8,8,256]{3,2,1,0:T(8,128)(2,1)} %bitcast.236) | data formatting | bytes 786432 | tf_op jit(solution)/shard_map/all_to_all | solution.py:44
  9.9 7.4 %all-to-all-done = bf16[96,8,256]{2,0,1:T(8,128)(2,1)S(1)} async-done(((bf16[96,8,256]{2,0,1:T(8,128)(2,1)}), bf16[96,8,256]{2,0,1:T(8,128)(2,1)S(1)}, u32[]{:S(2)}, u32[]{:S(2)}) %all-to-all-start) | async-done | bytes 393248 | tf_op jit(solution)/shard_map/all_to_all | solution.py:43
  17.3 6.1 %all-to-all-start.2 = ((bf16[96,8,256]{2,0,1:T(8,128)(2,1)}), bf16[96,8,256]{2,0,1:T(8,128)(2,1)S(1)}, u32[]{:S(2)}, u32[]{:S(2)}) async-start(bf16[96,8,256]{2,0,1:T(8,128)(2,1)} %bitcast.229), calls=%async_computation.2 | async-start | bytes 786432 | tf_op jit(solution)/shard_map/all_to_all | solution.py:44
  23.4 1.6 %fusion.88 = (s32[1]{0:T(128)}, s32[1]{0:T(128)}, s32[1]{0:T(128)}, s32[1]{0:T(128)}, s32[1]{0:T(128)}, /*index=5*/s32[1]{0:T(128)}, s32[1]{0:T(128)}, s32[1]{0:T(128)}) fusion(s32[8]{0:T(128)} %param.7, s32[]{:T(128)S(6)} %select_n.95, s32[]{:T(128)S(6)} %select_n.90, s32[]{:T(128)S(6)} %select_n.88, s32[]{:T(128)S(6)} %select_n.85, s32[]{:T(128)S(6)} %select_n.83, ...), kind=kLoop, calls=%fused_computation.129 | loop fusion | bytes 96 | tf_op jit(solution)/shard_map/jit(dynamic_index_in_dim)/dynamic_slice | solution.py:17
  28.8 2.1 %copy.133 = bf16[12,8,8,512]{3,2,0,1:T(8,128)(2,1)} copy(bf16[12,8,8,512]{3,2,1,0:T(8,128)(2,1)} %bitcast.234) | data formatting | bytes 1572864 | tf_op jit(solution)/shard_map/all_to_all | solution.py:42
  30.9 1.6 %all-to-all-done.2 = bf16[96,8,256]{2,0,1:T(8,128)(2,1)S(1)} async-done(((bf16[96,8,256]{2,0,1:T(8,128)(2,1)}), bf16[96,8,256]{2,0,1:T(8,128)(2,1)S(1)}, u32[]{:S(2)}, u32[]{:S(2)}) %all-to-all-start.2) | async-done | bytes 393248 | tf_op jit(solution)/shard_map/all_to_all | solution.py:44
  32.5 6.1 %all-to-all-start.1 = ((bf16[96,8,512]{2,0,1:T(8,128)(2,1)}), bf16[96,8,512]{2,0,1:T(8,128)(2,1)S(1)}, u32[]{:S(2)}, u32[]{:S(2)}) async-start(bf16[96,8,512]{2,0,1:T(8,128)(2,1)} %bitcast.227), calls=%async_computation.1 | async-start | bytes 1572864 | tf_op jit(solution)/shard_map/all_to_all | solution.py:42
  39.8 2.4 %broadcast_compare_fusion = (pred[768,384]{0,1:T(8,128)(4,1)S(1)}, pred[768,384]{0,1:T(8,128)(4,1)}, pred[768,384]{0,1:T(8,128)(4,1)S(1)}, pred[768,384]{0,1:T(8...) fusion(s32[768]{0:T(1024)S(1)} %pad_add_fusion, ...), kind=kLoop, calls=%fused_computation.49 | loop fusion | flops 2359296 | bytes 2374656 | tf_op jit(solution)/shard_map/le | solution.py:28
  42.4 0.9 fusion.87
  43.2 0.8 copy_dynamic-update-slice_fusion
  44.0 2.2 %collective-permute-start = (bf16[2,768,2,128]{3,1,2,0:T(8,128)(2,1)}, bf16[2,768,2,128]{3,1,2,0:T(8,128)(2,1)}, u32[]{:S(2)}, u32[]{:S(2)}) collective-permute-start(bf16[2,768,2,128]{3,1,2,0:T(8,128)(2,1)} %copy_dynamic-update-slice_fusion), channel_id=1, source_target_pairs={{0,1},{1,2},{2,3},{3,0},{4,5},{5,6},{6,7},{7,4},{8,9},{9,10},{10,1... | collective-permute-start | bytes 2359304 | tf_op jit(solution)/shard_map/while/body/eval_jaxpr/ppermute | solution.py:13
  46.9 10.7 %all-to-all-done.1 = bf16[96,8,512]{2,0,1:T(8,128)(2,1)S(1)} async-done(((bf16[96,8,512]{2,0,1:T(8,128)(2,1)}), bf16[96,8,512]{2,0,1:T(8,128)(2,1)S(1)}, u32[]{:S(2)}, u32[]{:S(2)}) %all-to-all-start.1) | async-done | bytes 786464 | tf_op jit(solution)/shard_map/all_to_all | solution.py:42
  57.8 2.8 %fusion = (f32[2,2,768]{2,1,0:T(2,128)S(1)}, f32[2,384,768,2]{2,1,3,0:T(8,128)S(1)}) fusion(pred[768,384]{0,1:T(8,128)(4,1)} %get-tuple-element.46, bf16[768,2,2,128]{3,2,1,0:T(2,128)(2,1)S(1)} %reshape.260, bf16[1,768,2,128]{3,1,2,0:T(8,128)(2,1)S(1)} %get-tuple-element.25), kind=kOutput, calls=%fused_computation.8 | convolution fusion | flops 306705408 | bytes 6008832 | tf_op jit(solution)/shard_map/rhgd,khd->hgrk/dot_general | solution.py:24
  60.6 1.8 %fusion.30 = f32[2,2,768,128]{2,3,1,0:T(8,128)S(1)} fusion(f32[2,384,768,2]{2,1,3,0:T(8,128)S(1)} %get-tuple-element.68, pred[768,384]{0,1:T(8,128)(4,1)S(1)} %copy-done.3, bf16[1,384,2,128]{1,3,2,0:T(8,128)(2,1)S(1)} %copy.90), kind=kOutput, calls=%fused_computation.31 | convolution fusion | flops 306708480 | bytes 6782976 | tf_op jit(solution)/shard_map/hgrk,khd->rhgd/dot_general | solution.py:31
  62.4 1.8 %fusion.2 = (f32[2,2,768]{2,1,0:T(2,128)S(1)}, f32[2,384,768,2]{2,1,3,0:T(8,128)S(1)}) fusion(pred[768,384]{0,1:T(8,128)(4,1)S(1)} %copy-done.2, bf16[768,2,2,128]{3,2,1,0:T(2,128)(2,1)S(1)} %reshape.260, bf16[1,768,2,128]{3,1,2,0:T(8,128)(2,1)S(1)} %get-tuple-element.25), kind=kOutput, calls=%fused_computation.10 | convolution fusion | flops 306705408 | bytes 6008832 | tf_op jit(solution)/shard_map/rhgd,khd->hgrk/dot_general | solution.py:24
  64.2 1.8 %fusion.28 = f32[2,2,768,128]{2,3,1,0:T(8,128)S(1)} fusion(f32[2,384,768,2]{2,1,3,0:T(8,128)S(1)} %get-tuple-element.70, pred[768,384]{0,1:T(8,128)(4,1)S(1)} %copy-done.2, bf16[1,384,2,128]{1,3,2,0:T(8,128)(2,1)S(1)} %copy.91), kind=kOutput, calls=%fused_computation.30 | convolution fusion | flops 306708480 | bytes 6782976 | tf_op jit(solution)/shard_map/hgrk,khd->rhgd/dot_general | solution.py:31
  66.0 3.5 %collective-permute-start.2 = (bf16[2,768,2,128]{3,1,2,0:T(8,128)(2,1)}, bf16[2,768,2,128]{3,1,2,0:T(8,128)(2,1)S(1)}, u32[]{:S(2)}, u32[]{:S(2)}) collective-permute-start(bf16[2,768,2,128]{3,1,2,0:T(8,128)(2,1)} %collective-permute-done), channel_id=1, source_target_pairs={{0,1},{1,2},{2,3},{3,0},{4,5},{5,6},{6,7},{7,4},{8,9},{9,10},{10,1... | collective-permute-start | bytes 2359304 | tf_op jit(solution)/shard_map/ppermute | solution.py:13
  69.5 2.7 %fusion.10 = (f32[2,2,768]{2,1,0:T(2,128)S(1)}, f32[2,384,768,2]{2,1,3,0:T(8,128)S(1)}) fusion(pred[768,384]{0,1:T(8,128)(4,1)S(1)} %copy-done.1, bf16[768,2,2,128]{3,2,1,0:T(2,128)(2,1)S(1)} %reshape.260, bf16[2,768,2,128]{3,1,2,0:T(8,128)(2,1)} %collective-permute-done.1), kind=kOutput, calls=%fused_computation.18 | convolution fusion | flops 306705408 | bytes 6008832 | tf_op jit(solution)/shard_map/while/body/eval_jaxpr/rhgd,khd->hgrk/dot_general | solution.py:24
  72.2 2.6 %fusion.20 = f32[2,128,2,768]{3,1,2,0:T(8,128)S(1)} fusion(f32[2,384,768,2]{2,1,3,0:T(8,128)S(1)} %get-tuple-element.60, pred[768,384]{0,1:T(8,128)(4,1)S(1)} %copy-done.1, bf16[2,768,2,128]{3,1,2,0:T(8,128)(2,1)} %collective-permute-done.1), kind=kOutput, calls=%fused_computation.26 | convolution fusion | flops 306708480 | bytes 6782976 | tf_op jit(solution)/shard_map/while/body/eval_jaxpr/hgrk,khd->rhgd/dot_general | solution.py:31
  74.8 2.7 %fusion.8 = (f32[2,2,768]{2,1,0:T(2,128)S(1)}, f32[2,384,768,2]{2,1,3,0:T(8,128)S(1)}) fusion(pred[768,384]{0,1:T(8,128)(4,1)S(1)} %copy-done, bf16[768,2,2,128]{3,2,1,0:T(2,128)(2,1)S(1)} %reshape.260, bf16[2,768,2,128]{3,1,2,0:T(8,128)(2,1)} %collective-permute-done.1), kind=kOutput, calls=%fused_computation.16 | convolution fusion | flops 306705408 | bytes 6008832 | tf_op jit(solution)/shard_map/while/body/eval_jaxpr/rhgd,khd->hgrk/dot_general | solution.py:24
  77.5 2.5 %fusion.22 = f32[2,128,2,768]{3,1,2,0:T(8,128)S(1)} fusion(f32[2,384,768,2]{2,1,3,0:T(8,128)S(1)} %get-tuple-element.62, pred[768,384]{0,1:T(8,128)(4,1)S(1)} %copy-done, bf16[2,768,2,128]{3,1,2,0:T(8,128)(2,1)} %collective-permute-done.1), kind=kOutput, calls=%fused_computation.27 | convolution fusion | flops 306708480 | bytes 6782976 | tf_op jit(solution)/shard_map/while/body/eval_jaxpr/hgrk,khd->rhgd/dot_general | solution.py:31
  80.1 2.7 %fusion.6 = (f32[2,2,768]{2,1,0:T(2,128)S(1)}, f32[2,384,768,2]{2,1,3,0:T(8,128)S(1)}) fusion(pred[768,384]{0,1:T(8,128)(4,1)S(1)} %get-tuple-element.40, bf16[768,2,2,128]{3,2,1,0:T(2,128)(2,1)S(1)} %reshape.260, bf16[2,768,2,128]{3,1,2,0:T(8,128)(2,1)} %collective-permute-done), kind=kOutput, calls=%fused_computation.14 | convolution fusion | flops 306705408 | bytes 6008832 | tf_op jit(solution)/shard_map/while/body/eval_jaxpr/rhgd,khd->hgrk/dot_general | solution.py:24
  82.8 2.5 %fusion.24 = f32[2,128,2,768]{3,1,2,0:T(8,128)S(1)} fusion(f32[2,384,768,2]{2,1,3,0:T(8,128)S(1)} %get-tuple-element.64, pred[768,384]{0,1:T(8,128)(4,1)S(1)} %get-tuple-element.40, bf16[2,768,2,128]{3,1,2,0:T(8,128)(2,1)} %collective-permute-done), kind=kOutput, calls=%fused_computation.28 | convolution fusion | flops 306708480 | bytes 6782976 | tf_op jit(solution)/shard_map/while/body/eval_jaxpr/hgrk,khd->rhgd/dot_general | solution.py:31
  85.3 2.7 %fusion.4 = (f32[2,2,768]{2,1,0:T(2,128)S(1)}, f32[2,384,768,2]{2,1,3,0:T(8,128)S(1)}) fusion(pred[768,384]{0,1:T(8,128)(4,1)S(1)} %get-tuple-element.29, bf16[768,2,2,128]{3,2,1,0:T(2,128)(2,1)S(1)} %reshape.260, bf16[2,768,2,128]{3,1,2,0:T(8,128)(2,1)} %collective-permute-done), kind=kOutput, calls=%fused_computation.12 | convolution fusion | flops 306705408 | bytes 6008832 | tf_op jit(solution)/shard_map/while/body/eval_jaxpr/rhgd,khd->hgrk/dot_general | solution.py:24
  88.1 2.7 %fusion.26 = f32[2,128,2,768]{3,1,2,0:T(8,128)S(1)} fusion(f32[2,384,768,2]{2,1,3,0:T(8,128)S(1)} %get-tuple-element.66, pred[768,384]{0,1:T(8,128)(4,1)S(1)} %get-tuple-element.29, bf16[2,768,2,128]{3,1,2,0:T(8,128)(2,1)} %collective-permute-done), kind=kOutput, calls=%fused_computation.29 | convolution fusion | flops 306708480 | bytes 6782976 | tf_op jit(solution)/shard_map/while/body/eval_jaxpr/hgrk,khd->rhgd/dot_general | solution.py:31
  90.8 1.8 %fusion.12 = (f32[2,2,768]{2,1,0:T(2,128)S(1)}, f32[2,384,768,2]{2,1,3,0:T(8,128)S(1)}) fusion(pred[768,384]{0,1:T(8,128)(4,1)S(1)} %get-tuple-element.45, bf16[768,2,2,128]{3,2,1,0:T(2,128)(2,1)S(1)} %reshape.260, bf16[2,768,2,128]{3,1,2,0:T(8,128)(2,1)S(1)} %collective-permute-done.2), kind=kOutput, calls=%fused_computation.20 | convolution fusion | flops 306705408 | bytes 6008832 | tf_op jit(solution)/shard_map/rhgd,khd->hgrk/dot_general | solution.py:24
  92.6 1.8 %fusion.14 = (f32[2,2,768]{2,1,0:T(2,128)S(1)}, f32[2,384,768,2]{2,1,3,0:T(8,128)S(1)}) fusion(pred[768,384]{0,1:T(8,128)(4,1)S(1)} %get-tuple-element.27, bf16[768,2,2,128]{3,2,1,0:T(2,128)(2,1)S(1)} %reshape.260, bf16[2,768,2,128]{3,1,2,0:T(8,128)(2,1)S(1)} %collective-permute-done.2), kind=kOutput, calls=%fused_computation.22 | convolution fusion | flops 306705408 | bytes 6008832 | tf_op jit(solution)/shard_map/rhgd,khd->hgrk/dot_general | solution.py:24
  94.4 1.6 %fusion.18 = f32[2,128,2,768]{3,1,2,0:T(8,128)S(1)} fusion(f32[2,384,768,2]{2,1,3,0:T(8,128)S(1)} %get-tuple-element.58, pred[768,384]{0,1:T(8,128)(4,1)S(1)} %get-tuple-element.45, bf16[2,768,2,128]{3,1,2,0:T(8,128)(2,1)S(1)} %collective-permute-done.2), kind=kOutput, calls=%fused_computation.25 | convolution fusion | flops 306708480 | bytes 6782976 | tf_op jit(solution)/shard_map/hgrk,khd->rhgd/dot_general | solution.py:31
  96.1 2.0 %fusion.41 = bf16[768,2,2,128]{0,3,2,1:T(8,128)(2,1)S(1)} fusion(f32[2,128,2,768]{3,1,2,0:T(8,128)S(1)} %fusion.18, f32[2,128,2,768]{3,1,2,0:T(8,128)S(1)} %fusion.20, f32[2,128,2,768]{3,1,2,0:T(8,128)S(1)} %fusion.22, f32[2,128,2,768]{3,1,2,0:T(8,128)S(1)} %fusion.24, f32[2,128,2,768]{3,1,2,0:T(8,128)S(1)} %fusion.26, f32[2,2,768,128]{2,3,1,0:T(8,128)S(1)} %fusion.30, ...), kind=kOutput, calls=%fused_computation.42 | convolution fusion | flops 310247424 | bytes 17018880 | tf_op jit(solution)/shard_map/hgrk,khd->rhgd/dot_general | solution.py:31
  98.1 1.2 %copy.53 = bf16[768,512]{1,0:T(8,128)(2,1)} copy(bf16[768,512]{0,1:T(8,128)(2,1)S(1)} %bitcast.230) | data formatting | bytes 1572864 | tf_op jit(solution)/shard_map/convert_element_type | solution.py:104
  (24 shorter events, 1.1 us)
Async XLA Ops:
  1.8 15.5 %all-to-all-start = ((bf16[96,8,256]{2,0,1:T(8,128)(2,1)}), bf16[96,8,256]{2,0,1:T(8,128)(2,1)S(1)}, u32[]{:S(2)}, u32[]{:S(2)}) async-start(bf16[96,8,256]{2,0,1:T(8,128)(2,1)} %bitcast.228), calls=%async_computation | async-start | bytes 786432 | tf_op jit(solution)/shard_map/all_to_all | solution.py:43
  17.3 15.2 %all-to-all-start.2 = ((bf16[96,8,256]{2,0,1:T(8,128)(2,1)}), bf16[96,8,256]{2,0,1:T(8,128)(2,1)S(1)}, u32[]{:S(2)}, u32[]{:S(2)}) async-start(bf16[96,8,256]{2,0,1:T(8,128)(2,1)} %bitcast.229), calls=%async_computation.2 | async-start | bytes 786432 | tf_op jit(solution)/shard_map/all_to_all | solution.py:44
  32.5 25.1 %all-to-all-start.1 = ((bf16[96,8,512]{2,0,1:T(8,128)(2,1)}), bf16[96,8,512]{2,0,1:T(8,128)(2,1)S(1)}, u32[]{:S(2)}, u32[]{:S(2)}) async-start(bf16[96,8,512]{2,0,1:T(8,128)(2,1)} %bitcast.227), calls=%async_computation.1 | async-start | bytes 1572864 | tf_op jit(solution)/shard_map/all_to_all | solution.py:42
  44.0 22.0 %collective-permute-start = (bf16[2,768,2,128]{3,1,2,0:T(8,128)(2,1)}, bf16[2,768,2,128]{3,1,2,0:T(8,128)(2,1)}, u32[]{:S(2)}, u32[]{:S(2)}) collective-permute-start(bf16[2,768,2,128]{3,1,2,0:T(8,128)(2,1)} %copy_dynamic-update-slice_fusion), channel_id=1, source_target_pairs={{0,1},{1,2},{2,3},{3,0},{4,5},{5,6},{6,7},{7,4},{8,9},{9,10},{10,1... | collective-permute-start | bytes 2359304 | tf_op jit(solution)/shard_map/while/body/eval_jaxpr/ppermute | solution.py:13
  46.3 23.2 %collective-permute-start.1 = (bf16[2,768,2,128]{3,1,2,0:T(8,128)(2,1)}, bf16[2,768,2,128]{3,1,2,0:T(8,128)(2,1)}, u32[]{:S(2)}, u32[]{:S(2)}) collective-permute-start(bf16[2,768,2,128]{3,1,2,0:T(8,128)(2,1)} %copy_dynamic-update-slice_fusion), channel_id=1, source_target_pairs={{0,3},{1,0},{2,1},{3,2},{4,7},{5,4},{6,5},{7,6},{8,11},{9,8},{10,9... | collective-permute-start | bytes 2359304 | tf_op jit(solution)/shard_map/while/body/eval_jaxpr/ppermute | solution.py:13
  57.8 2.8 %copy-start.3 = (pred[768,384]{0,1:T(8,128)(4,1)S(1)}, pred[768,384]{0,1:T(8,128)(4,1)}, u32[]{:S(2)}) copy-start(pred[768,384]{0,1:T(8,128)(4,1)} %get-tuple-element.46) | copy-start | bytes 884740
  60.6 1.8 %copy-start.2 = (pred[768,384]{0,1:T(8,128)(4,1)S(1)}, pred[768,384]{0,1:T(8,128)(4,1)}, u32[]{:S(2)}) copy-start(pred[768,384]{0,1:T(8,128)(4,1)} %get-tuple-element.28) | copy-start | bytes 884740
  64.2 5.3 %copy-start.1 = (pred[768,384]{0,1:T(8,128)(4,1)S(1)}, pred[768,384]{0,1:T(8,128)(4,1)}, u32[]{:S(2)}) copy-start(pred[768,384]{0,1:T(8,128)(4,1)} %get-tuple-element.44) | copy-start | bytes 884740
  66.0 24.8 %collective-permute-start.2 = (bf16[2,768,2,128]{3,1,2,0:T(8,128)(2,1)}, bf16[2,768,2,128]{3,1,2,0:T(8,128)(2,1)S(1)}, u32[]{:S(2)}, u32[]{:S(2)}) collective-permute-start(bf16[2,768,2,128]{3,1,2,0:T(8,128)(2,1)} %collective-permute-done), channel_id=1, source_target_pairs={{0,1},{1,2},{2,3},{3,0},{4,5},{5,6},{6,7},{7,4},{8,9},{9,10},{10,1... | collective-permute-start | bytes 2359304 | tf_op jit(solution)/shard_map/ppermute | solution.py:13
  72.2 2.6 %copy-start = (pred[768,384]{0,1:T(8,128)(4,1)S(1)}, pred[768,384]{0,1:T(8,128)(4,1)}, u32[]{:S(2)}) copy-start(pred[768,384]{0,1:T(8,128)(4,1)} %get-tuple-element.42) | copy-start | bytes 884740
where the time goes:
time: 100 us; the launch traced here: 99.2 us
  matrix products  36.6 us (37%)
  starting transfers between devices  24.2 us (24%)
  waiting for transfers between devices  19.7 us (20%)
  local copies, waits for them, and re-layouts  11.1 us (11%)
  between operations  5.27 us (5%)
  other arithmetic  2.43 us (2%)
    dot_general x8, matrix products, add_block(): jnp.einsum('rhgd,khd->hgrk', query_rows, key_block, preferred_element_typ...  19 us
    dot_general x8, matrix products, add_block(): jnp.einsum('hgrk,khd->rhgd', weights.astype(jnp.bfloat16), value_block, p...  17.6 us
    all_to_all x1, waiting for transfers between devices, shards(): lax.all_to_all(query, 'head', split_axis=1, concat_axis=0, tiled=True)  10.7 us
    all_to_all x1, waiting for transfers between devices, shards(): lax.all_to_all(key, 'head', split_axis=1, concat_axis=0, tiled=True)  7.41 us
    all_to_all x1, starting transfers between devices, shards(): lax.all_to_all(key, 'head', split_axis=1, concat_axis=0, tiled=True)  6.37 us
    all_to_all x1, starting transfers between devices, shards(): lax.all_to_all(query, 'head', split_axis=1, concat_axis=0, tiled=True)  6.06 us
    all_to_all x1, starting transfers between devices, shards(): lax.all_to_all(value, 'head', split_axis=1, concat_axis=0, tiled=True)  6.06 us
    ppermute x3, starting transfers between devices, from_behind(): lax.ppermute(value, axis, [(i, (i + by) % size) for i in range(size)])  5.67 us
  transfers between devices with their start and end apart: 6, of which 3 were waited for; matrix products, arithmetic and copies ran while one was open for 40% of the time, Pallas kernels for 0%

commit v1 on v0

--- a/solution.py
+++ b/solution.py
@@ -41,7 +41,12 @@
     query, key, value = (
         lax.all_to_all(query, "head", split_axis=1, concat_axis=0, tiled=True),
         lax.all_to_all(key, "head", split_axis=1, concat_axis=0, tiled=True),
-        lax.all_to_all(value, "head", split_axis=1, concat_axis=0, tiled=True),
+        jnp.concatenate(
+            lax.all_to_all(
+                jnp.stack(jnp.split(value, lax.axis_size("head"), axis=1)), "head", 0, 0
+            ),
+            axis=0,
+        ),
     )
     row_count = query.shape[0]
     block_len = row_count // 2

time: 100 us -> 102 us (1.020)
  local copies, waits for them, and re-layouts: 11.1 us -> 20.7 us
  waiting for transfers between devices: 19.7 us -> 12.2 us
    unnamed x10 -> x17, local copies, waits for them, and re-layouts: 0.37 us -> 10.3 us
    all_to_all x1, waiting for transfers between devices: 7.41 us -> 0.01 us  [shards(): lax.all_to_all(key, 'head', split_axis=1, concat_axis=0, tiled=True)]
    all_to_all x1 -> x0, local copies, waits for them, and re-layouts: 1.76 us -> none  [shards(): lax.all_to_all(value, 'head', split_axis=1, concat_axis=0, tiled=True)]
    another operation x0 -> x1, local copies, waits for them, and re-layouts: none -> 1.41 us  [shards(): jnp.stack(jnp.split(value, lax.axis_size('head'), axis=1))]
  transfers between devices with their start and end apart: 6 -> 6, of which waited for: 3 -> 2; matrix products, arithmetic and copies ran while one was open for 40% -> 49% of each run, Pallas kernels for 0% -> 0%
where the time goes in v1:
time: 102 us; the launch traced here: 101 us
  matrix products  36.6 us (36%)
  starting transfers between devices  23.6 us (23%)
  local copies, waits for them, and re-layouts  20.7 us (20%)
  waiting for transfers between devices  12.2 us (12%)
  between operations  5.27 us (5%)
  other arithmetic  2.43 us (2%)
    dot_general x8, matrix products, add_block(): jnp.einsum('rhgd,khd->hgrk', query_rows, key_block, preferred_element_typ...  19 us
    dot_general x8, matrix products, add_block(): jnp.einsum('hgrk,khd->rhgd', weights.astype(jnp.bfloat16), value_block, p...  17.6 us
    all_to_all x1, waiting for transfers between devices, shards(): lax.all_to_all(query, 'head', split_axis=1, concat_axis=0, tiled=True)  10.6 us
    unnamed x17, local copies, waits for them, and re-layouts  10.3 us
    all_to_all x1, starting transfers between devices, shards(): lax.all_to_all(key, 'head', split_axis=1, concat_axis=0, tiled=True)  6.37 us
    all_to_all x1, starting transfers between devices, shards(): lax.all_to_all(query, 'head', split_axis=1, concat_axis=0, tiled=True)  6.02 us
    ppermute x3, starting transfers between devices, from_behind(): lax.ppermute(value, axis, [(i, (i + by) % size) for i in range(size)])  5.77 us
    all_to_all x1, starting transfers between devices, shards(): lax.all_to_all(jnp.stack(jnp.split(value, lax.axis_size('head'), axis=1))...  5.44 us
  transfers between devices with their start and end apart: 6, of which 2 were waited for; matrix products, arithmetic and copies ran while one was open for 49% of the time, Pallas kernels for 0%

profile of v1, /device:TPU:1, one launch (start us, length us, event | category | flops | bytes accessed | tf_op | source)
XLA Modules:
  0.0 100.8 jit_solution(12166987249404651843)
XLA Ops:
  0.0 1.8 %copy.131 = bf16[12,8,8,256]{3,2,0,1:T(8,128)(2,1)} copy(bf16[12,8,8,256]{3,2,1,0:T(8,128)(2,1)} %bitcast.223) | data formatting | bytes 786432 | tf_op jit(solution)/shard_map/all_to_all | solution.py:43
  1.8 6.4 %all-to-all-start.1 = ((bf16[96,8,256]{2,0,1:T(8,128)(2,1)}), bf16[96,8,256]{2,0,1:T(8,128)(2,1)S(1)}, u32[]{:S(2)}, u32[]{:S(2)}) async-start(bf16[96,8,256]{2,0,1:T(8,128)(2,1)} %bitcast.218), calls=%async_computation.1 | async-start | bytes 786432 | tf_op jit(solution)/shard_map/all_to_all | solution.py:43
  8.1 1.4 %bitcast_dynamic-update-slice_fusion.7 = bf16[8,96,256]{2,1,0:T(8,128)(2,1)} fusion(bf16[96,2048]{1,0:T(8,128)(2,1)} %param.6), kind=kLoop, calls=%fused_computation.92 | loop fusion | bytes 98304
  9.6 1.4 %bitcast_dynamic-update-slice_fusion.6 = bf16[8,96,256]{2,1,0:T(8,128)(2,1)} fusion(bf16[8,96,256]{2,1,0:T(8,128)(2,1)} %bitcast_dynamic-update-slice_fusion.7, bf16[96,2048]{1,0:T(8,128)(2,1)} %param.6), kind=kLoop, calls=%fused_computation.91 | loop fusion | bytes 98304
  11.0 1.4 %bitcast_dynamic-update-slice_fusion.5 = bf16[8,96,256]{2,1,0:T(8,128)(2,1)} fusion(bf16[8,96,256]{2,1,0:T(8,128)(2,1)} %bitcast_dynamic-update-slice_fusion.6, bf16[96,2048]{1,0:T(8,128)(2,1)} %param.6), kind=kLoop, calls=%fused_computation.90 | loop fusion | bytes 98304
  13.8 1.4 %bitcast_dynamic-update-slice_fusion.3 = bf16[8,96,256]{2,1,0:T(8,128)(2,1)} fusion(bf16[8,96,256]{2,1,0:T(8,128)(2,1)} %bitcast_dynamic-update-slice_fusion.4, bf16[96,2048]{1,0:T(8,128)(2,1)} %param.6), kind=kLoop, calls=%fused_computation.88 | loop fusion | bytes 98304
  16.6 1.4 %bitcast_dynamic-update-slice_fusion.1 = bf16[8,96,256]{2,1,0:T(8,128)(2,1)} fusion(bf16[8,96,256]{2,1,0:T(8,128)(2,1)} %bitcast_dynamic-update-slice_fusion.2, bf16[96,2048]{1,0:T(8,128)(2,1)} %param.6), kind=kLoop, calls=%fused_computation.86 | loop fusion | bytes 98304
  19.5 5.4 %all-to-all-start = ((bf16[8,96,256]{2,1,0:T(8,128)(2,1)}), bf16[8,96,256]{2,1,0:T(8,128)(2,1)S(1)}, u32[]{:S(2)}, u32[]{:S(2)}) async-start(bf16[8,96,256]{2,1,0:T(8,128)(2,1)} %bitcast_dynamic-update-slice_fusion), calls=%async_computation | async-start | bytes 786432 | tf_op jit(solution)/shard_map/all_to_all | solution.py:45
  24.9 1.6 %fusion.87 = (s32[1]{0:T(128)}, s32[1]{0:T(128)}, s32[1]{0:T(128)}, s32[1]{0:T(128)}, s32[1]{0:T(128)}, /*index=5*/s32[1]{0:T(128)}, s32[1]{0:T(128)}, s32[1]{0:T(128)}) fusion(s32[8]{0:T(128)} %param.7, s32[]{:T(128)S(6)} %select_n.95, s32[]{:T(128)S(6)} %select_n.90, s32[]{:T(128)S(6)} %select_n.88, s32[]{:T(128)S(6)} %select_n.85, s32[]{:T(128)S(6)} %select_n.83, ...), kind=kLoop, calls=%fused_computation.130 | loop fusion | bytes 96 | tf_op jit(solution)/shard_map/jit(dynamic_index_in_dim)/dynamic_slice | solution.py:17
  30.3 2.1 %copy.130 = bf16[12,8,8,512]{3,2,0,1:T(8,128)(2,1)} copy(bf16[12,8,8,512]{3,2,1,0:T(8,128)(2,1)} %bitcast.222) | data formatting | bytes 1572864 | tf_op jit(solution)/shard_map/all_to_all | solution.py:42
  32.4 1.6 %all-to-all-done = bf16[8,96,256]{2,1,0:T(8,128)(2,1)S(1)} async-done(((bf16[8,96,256]{2,1,0:T(8,128)(2,1)}), bf16[8,96,256]{2,1,0:T(8,128)(2,1)S(1)}, u32[]{:S(2)}, u32[]{:S(2)}) %all-to-all-start) | async-done | bytes 393248 | tf_op jit(solution)/shard_map/all_to_all | solution.py:45
  34.0 6.0 %all-to-all-start.2 = ((bf16[96,8,512]{2,0,1:T(8,128)(2,1)}), bf16[96,8,512]{2,0,1:T(8,128)(2,1)S(1)}, u32[]{:S(2)}, u32[]{:S(2)}) async-start(bf16[96,8,512]{2,0,1:T(8,128)(2,1)} %bitcast.217), calls=%async_computation.2 | async-start | bytes 1572864 | tf_op jit(solution)/shard_map/all_to_all | solution.py:42
  41.3 2.4 %broadcast_compare_fusion = (pred[768,384]{0,1:T(8,128)(4,1)S(1)}, pred[768,384]{0,1:T(8,128)(4,1)}, pred[768,384]{0,1:T(8,128)(4,1)S(1)}, pred[768,384]{0,1:T(8...) fusion(s32[768]{0:T(1024)S(1)} %pad_add_fusion, ...), kind=kLoop, calls=%fused_computation.43 | loop fusion | flops 2359296 | bytes 2374656 | tf_op jit(solution)/shard_map/le | solution.py:28
  45.6 2.3 %collective-permute-start = (bf16[2,768,2,128]{3,1,2,0:T(8,128)(2,1)}, bf16[2,768,2,128]{3,1,2,0:T(8,128)(2,1)}, u32[]{:S(2)}, u32[]{:S(2)}) collective-permute-start(bf16[2,768,2,128]{3,1,2,0:T(8,128)(2,1)} %copy_dynamic-update-slice_fusion), channel_id=1, source_target_pairs={{0,1},{1,2},{2,3},{3,0},{4,5},{5,6},{6,7},{7,4},{8,9},{9,10},{10,1... | collective-permute-start | bytes 2359304 | tf_op jit(solution)/shard_map/while/body/eval_jaxpr/ppermute | solution.py:13
  48.5 10.6 %all-to-all-done.2 = bf16[96,8,512]{2,0,1:T(8,128)(2,1)S(1)} async-done(((bf16[96,8,512]{2,0,1:T(8,128)(2,1)}), bf16[96,8,512]{2,0,1:T(8,128)(2,1)S(1)}, u32[]{:S(2)}, u32[]{:S(2)}) %all-to-all-start.2) | async-done | bytes 786464 | tf_op jit(solution)/shard_map/all_to_all | solution.py:42
  59.3 2.8 %fusion = (f32[2,2,768]{2,1,0:T(2,128)S(1)}, f32[2,384,768,2]{2,1,3,0:T(8,128)S(1)}) fusion(pred[768,384]{0,1:T(8,128)(4,1)} %get-tuple-element.46, bf16[768,2,2,128]{3,2,1,0:T(2,128)(2,1)S(1)} %reshape.256, bf16[1,768,2,128]{3,1,2,0:T(8,128)(2,1)S(1)} %get-tuple-element.25), kind=kOutput, calls=%fused_computation.8 | convolution fusion | flops 306705408 | bytes 6008832 | tf_op jit(solution)/shard_map/rhgd,khd->hgrk/dot_general | solution.py:24
  62.1 1.8 %fusion.30 = f32[2,128,2,768]{3,1,2,0:T(8,128)S(1)} fusion(f32[2,384,768,2]{2,1,3,0:T(8,128)S(1)} %get-tuple-element.68, pred[768,384]{0,1:T(8,128)(4,1)S(1)} %copy-done.3, bf16[1,384,2,128]{1,3,2,0:T(8,128)(2,1)S(1)} %copy.89), kind=kOutput, calls=%fused_computation.31 | convolution fusion | flops 306708480 | bytes 6782976 | tf_op jit(solution)/shard_map/hgrk,khd->rhgd/dot_general | solution.py:31
  63.9 1.8 %fusion.2 = (f32[2,2,768]{2,1,0:T(2,128)S(1)}, f32[2,384,768,2]{2,1,3,0:T(8,128)S(1)}) fusion(pred[768,384]{0,1:T(8,128)(4,1)S(1)} %copy-done.2, bf16[768,2,2,128]{3,2,1,0:T(2,128)(2,1)S(1)} %reshape.256, bf16[1,768,2,128]{3,1,2,0:T(8,128)(2,1)S(1)} %get-tuple-element.25), kind=kOutput, calls=%fused_computation.10 | convolution fusion | flops 306705408 | bytes 6008832 | tf_op jit(solution)/shard_map/rhgd,khd->hgrk/dot_general | solution.py:24
  65.7 1.8 %fusion.28 = f32[2,128,2,768]{3,1,2,0:T(8,128)S(1)} fusion(f32[2,384,768,2]{2,1,3,0:T(8,128)S(1)} %get-tuple-element.70, pred[768,384]{0,1:T(8,128)(4,1)S(1)} %copy-done.2, bf16[1,384,2,128]{1,3,2,0:T(8,128)(2,1)S(1)} %copy.90), kind=kOutput, calls=%fused_computation.30 | convolution fusion | flops 306708480 | bytes 6782976 | tf_op jit(solution)/shard_map/hgrk,khd->rhgd/dot_general | solution.py:31
  67.5 3.5 %collective-permute-start.2 = (bf16[2,768,2,128]{3,1,2,0:T(8,128)(2,1)}, bf16[2,768,2,128]{3,1,2,0:T(8,128)(2,1)S(1)}, u32[]{:S(2)}, u32[]{:S(2)}) collective-permute-start(bf16[2,768,2,128]{3,1,2,0:T(8,128)(2,1)} %collective-permute-done), channel_id=1, source_target_pairs={{0,1},{1,2},{2,3},{3,0},{4,5},{5,6},{6,7},{7,4},{8,9},{9,10},{10,1... | collective-permute-start | bytes 2359304 | tf_op jit(solution)/shard_map/ppermute | solution.py:13
  71.0 2.7 %fusion.10 = (f32[2,2,768]{2,1,0:T(2,128)S(1)}, f32[2,384,768,2]{2,1,3,0:T(8,128)S(1)}) fusion(pred[768,384]{0,1:T(8,128)(4,1)S(1)} %copy-done.1, bf16[768,2,2,128]{3,2,1,0:T(2,128)(2,1)S(1)} %reshape.256, bf16[2,768,2,128]{3,1,2,0:T(8,128)(2,1)} %collective-permute-done.1), kind=kOutput, calls=%fused_computation.18 | convolution fusion | flops 306705408 | bytes 6008832 | tf_op jit(solution)/shard_map/while/body/eval_jaxpr/rhgd,khd->hgrk/dot_general | solution.py:24
  73.7 2.6 %fusion.20 = f32[2,128,2,768]{3,1,2,0:T(8,128)S(1)} fusion(f32[2,384,768,2]{2,1,3,0:T(8,128)S(1)} %get-tuple-element.60, pred[768,384]{0,1:T(8,128)(4,1)S(1)} %copy-done.1, bf16[2,768,2,128]{3,1,2,0:T(8,128)(2,1)} %collective-permute-done.1), kind=kOutput, calls=%fused_computation.26 | convolution fusion | flops 306708480 | bytes 6782976 | tf_op jit(solution)/shard_map/while/body/eval_jaxpr/hgrk,khd->rhgd/dot_general | solution.py:31
  76.3 2.7 %fusion.8 = (f32[2,2,768]{2,1,0:T(2,128)S(1)}, f32[2,384,768,2]{2,1,3,0:T(8,128)S(1)}) fusion(pred[768,384]{0,1:T(8,128)(4,1)S(1)} %copy-done, bf16[768,2,2,128]{3,2,1,0:T(2,128)(2,1)S(1)} %reshape.256, bf16[2,768,2,128]{3,1,2,0:T(8,128)(2,1)} %collective-permute-done.1), kind=kOutput, calls=%fused_computation.16 | convolution fusion | flops 306705408 | bytes 6008832 | tf_op jit(solution)/shard_map/while/body/eval_jaxpr/rhgd,khd->hgrk/dot_general | solution.py:24
  79.1 2.5 %fusion.22 = f32[2,128,2,768]{3,1,2,0:T(8,128)S(1)} fusion(f32[2,384,768,2]{2,1,3,0:T(8,128)S(1)} %get-tuple-element.62, pred[768,384]{0,1:T(8,128)(4,1)S(1)} %copy-done, bf16[2,768,2,128]{3,1,2,0:T(8,128)(2,1)} %collective-permute-done.1), kind=kOutput, calls=%fused_computation.27 | convolution fusion | flops 306708480 | bytes 6782976 | tf_op jit(solution)/shard_map/while/body/eval_jaxpr/hgrk,khd->rhgd/dot_general | solution.py:31
  81.6 2.7 %fusion.6 = (f32[2,2,768]{2,1,0:T(2,128)S(1)}, f32[2,384,768,2]{2,1,3,0:T(8,128)S(1)}) fusion(pred[768,384]{0,1:T(8,128)(4,1)S(1)} %get-tuple-element.40, bf16[768,2,2,128]{3,2,1,0:T(2,128)(2,1)S(1)} %reshape.256, bf16[2,768,2,128]{3,1,2,0:T(8,128)(2,1)} %collective-permute-done), kind=kOutput, calls=%fused_computation.14 | convolution fusion | flops 306705408 | bytes 6008832 | tf_op jit(solution)/shard_map/while/body/eval_jaxpr/rhgd,khd->hgrk/dot_general | solution.py:24
  84.3 2.5 %fusion.24 = f32[2,128,2,768]{3,1,2,0:T(8,128)S(1)} fusion(f32[2,384,768,2]{2,1,3,0:T(8,128)S(1)} %get-tuple-element.64, pred[768,384]{0,1:T(8,128)(4,1)S(1)} %get-tuple-element.40, bf16[2,768,2,128]{3,1,2,0:T(8,128)(2,1)} %collective-permute-done), kind=kOutput, calls=%fused_computation.28 | convolution fusion | flops 306708480 | bytes 6782976 | tf_op jit(solution)/shard_map/while/body/eval_jaxpr/hgrk,khd->rhgd/dot_general | solution.py:31
  86.9 2.7 %fusion.4 = (f32[2,2,768]{2,1,0:T(2,128)S(1)}, f32[2,384,768,2]{2,1,3,0:T(8,128)S(1)}) fusion(pred[768,384]{0,1:T(8,128)(4,1)S(1)} %get-tuple-element.29, bf16[768,2,2,128]{3,2,1,0:T(2,128)(2,1)S(1)} %reshape.256, bf16[2,768,2,128]{3,1,2,0:T(8,128)(2,1)} %collective-permute-done), kind=kOutput, calls=%fused_computation.12 | convolution fusion | flops 306705408 | bytes 6008832 | tf_op jit(solution)/shard_map/while/body/eval_jaxpr/rhgd,khd->hgrk/dot_general | solution.py:24
  89.6 2.7 %fusion.26 = f32[2,128,2,768]{3,1,2,0:T(8,128)S(1)} fusion(f32[2,384,768,2]{2,1,3,0:T(8,128)S(1)} %get-tuple-element.66, pred[768,384]{0,1:T(8,128)(4,1)S(1)} %get-tuple-element.29, bf16[2,768,2,128]{3,1,2,0:T(8,128)(2,1)} %collective-permute-done), kind=kOutput, calls=%fused_computation.29 | convolution fusion | flops 306708480 | bytes 6782976 | tf_op jit(solution)/shard_map/while/body/eval_jaxpr/hgrk,khd->rhgd/dot_general | solution.py:31
  92.3 1.8 %fusion.12 = (f32[2,2,768]{2,1,0:T(2,128)S(1)}, f32[2,384,768,2]{2,1,3,0:T(8,128)S(1)}) fusion(pred[768,384]{0,1:T(8,128)(4,1)S(1)} %get-tuple-element.45, bf16[768,2,2,128]{3,2,1,0:T(2,128)(2,1)S(1)} %reshape.256, bf16[2,768,2,128]{3,1,2,0:T(8,128)(2,1)S(1)} %collective-permute-done.2), kind=kOutput, calls=%fused_computation.20 | convolution fusion | flops 306705408 | bytes 6008832 | tf_op jit(solution)/shard_map/rhgd,khd->hgrk/dot_general | solution.py:24
  94.1 1.8 %fusion.14 = (f32[2,2,768]{2,1,0:T(2,128)S(1)}, f32[2,384,768,2]{2,1,3,0:T(8,128)S(1)}) fusion(pred[768,384]{0,1:T(8,128)(4,1)S(1)} %get-tuple-element.27, bf16[768,2,2,128]{3,2,1,0:T(2,128)(2,1)S(1)} %reshape.256, bf16[2,768,2,128]{3,1,2,0:T(8,128)(2,1)S(1)} %collective-permute-done.2), kind=kOutput, calls=%fused_computation.22 | convolution fusion | flops 306705408 | bytes 6008832 | tf_op jit(solution)/shard_map/rhgd,khd->hgrk/dot_general | solution.py:24
  96.0 1.6 %fusion.18 = f32[2,128,2,768]{3,1,2,0:T(8,128)S(1)} fusion(f32[2,384,768,2]{2,1,3,0:T(8,128)S(1)} %get-tuple-element.58, pred[768,384]{0,1:T(8,128)(4,1)S(1)} %get-tuple-element.45, bf16[2,768,2,128]{3,1,2,0:T(8,128)(2,1)S(1)} %collective-permute-done.2), kind=kOutput, calls=%fused_computation.25 | convolution fusion | flops 306708480 | bytes 6782976 | tf_op jit(solution)/shard_map/hgrk,khd->rhgd/dot_general | solution.py:31
  97.6 2.0 %fusion.40 = bf16[768,2,2,128]{0,3,2,1:T(8,128)(2,1)S(1)} fusion(f32[2,128,2,768]{3,1,2,0:T(8,128)S(1)} %fusion.18, f32[2,128,2,768]{3,1,2,0:T(8,128)S(1)} %fusion.20, f32[2,128,2,768]{3,1,2,0:T(8,128)S(1)} %fusion.22, f32[2,128,2,768]{3,1,2,0:T(8,128)S(1)} %fusion.24, f32[2,128,2,768]{3,1,2,0:T(8,128)S(1)} %fusion.26, f32[2,128,2,768]{3,1,2,0:T(8,128)S(1)} %fusion.30, ...), kind=kOutput, calls=%fused_computation.41 | convolution fusion | flops 310247424 | bytes 17018880 | tf_op jit(solution)/shard_map/hgrk,khd->rhgd/dot_general | solution.py:31
  (31 shorter events, 8.2 us)
Async XLA Ops:
  1.8 17.7 %all-to-all-start.1 = ((bf16[96,8,256]{2,0,1:T(8,128)(2,1)}), bf16[96,8,256]{2,0,1:T(8,128)(2,1)S(1)}, u32[]{:S(2)}, u32[]{:S(2)}) async-start(bf16[96,8,256]{2,0,1:T(8,128)(2,1)} %bitcast.218), calls=%async_computation.1 | async-start | bytes 786432 | tf_op jit(solution)/shard_map/all_to_all | solution.py:43
  19.5 14.6 %all-to-all-start = ((bf16[8,96,256]{2,1,0:T(8,128)(2,1)}), bf16[8,96,256]{2,1,0:T(8,128)(2,1)S(1)}, u32[]{:S(2)}, u32[]{:S(2)}) async-start(bf16[8,96,256]{2,1,0:T(8,128)(2,1)} %bitcast_dynamic-update-slice_fusion), calls=%async_computation | async-start | bytes 786432 | tf_op jit(solution)/shard_map/all_to_all | solution.py:45
  34.0 25.0 %all-to-all-start.2 = ((bf16[96,8,512]{2,0,1:T(8,128)(2,1)}), bf16[96,8,512]{2,0,1:T(8,128)(2,1)S(1)}, u32[]{:S(2)}, u32[]{:S(2)}) async-start(bf16[96,8,512]{2,0,1:T(8,128)(2,1)} %bitcast.217), calls=%async_computation.2 | async-start | bytes 1572864 | tf_op jit(solution)/shard_map/all_to_all | solution.py:42
  45.6 21.9 %collective-permute-start = (bf16[2,768,2,128]{3,1,2,0:T(8,128)(2,1)}, bf16[2,768,2,128]{3,1,2,0:T(8,128)(2,1)}, u32[]{:S(2)}, u32[]{:S(2)}) collective-permute-start(bf16[2,768,2,128]{3,1,2,0:T(8,128)(2,1)} %copy_dynamic-update-slice_fusion), channel_id=1, source_target_pairs={{0,1},{1,2},{2,3},{3,0},{4,5},{5,6},{6,7},{7,4},{8,9},{9,10},{10,1... | collective-permute-start | bytes 2359304 | tf_op jit(solution)/shard_map/while/body/eval_jaxpr/ppermute | solution.py:13
  47.8 23.2 %collective-permute-start.1 = (bf16[2,768,2,128]{3,1,2,0:T(8,128)(2,1)}, bf16[2,768,2,128]{3,1,2,0:T(8,128)(2,1)}, u32[]{:S(2)}, u32[]{:S(2)}) collective-permute-start(bf16[2,768,2,128]{3,1,2,0:T(8,128)(2,1)} %copy_dynamic-update-slice_fusion), channel_id=1, source_target_pairs={{0,3},{1,0},{2,1},{3,2},{4,7},{5,4},{6,5},{7,6},{8,11},{9,8},{10,9... | collective-permute-start | bytes 2359304 | tf_op jit(solution)/shard_map/while/body/eval_jaxpr/ppermute | solution.py:13
  59.3 2.8 %copy-start.3 = (pred[768,384]{0,1:T(8,128)(4,1)S(1)}, pred[768,384]{0,1:T(8,128)(4,1)}, u32[]{:S(2)}) copy-start(pred[768,384]{0,1:T(8,128)(4,1)} %get-tuple-element.46) | copy-start | bytes 884740
  62.1 1.8 %copy-start.2 = (pred[768,384]{0,1:T(8,128)(4,1)S(1)}, pred[768,384]{0,1:T(8,128)(4,1)}, u32[]{:S(2)}) copy-start(pred[768,384]{0,1:T(8,128)(4,1)} %get-tuple-element.28) | copy-start | bytes 884740
  65.7 5.3 %copy-start.1 = (pred[768,384]{0,1:T(8,128)(4,1)S(1)}, pred[768,384]{0,1:T(8,128)(4,1)}, u32[]{:S(2)}) copy-start(pred[768,384]{0,1:T(8,128)(4,1)} %get-tuple-element.44) | copy-start | bytes 884740
  67.5 24.8 %collective-permute-start.2 = (bf16[2,768,2,128]{3,1,2,0:T(8,128)(2,1)}, bf16[2,768,2,128]{3,1,2,0:T(8,128)(2,1)S(1)}, u32[]{:S(2)}, u32[]{:S(2)}) collective-permute-start(bf16[2,768,2,128]{3,1,2,0:T(8,128)(2,1)} %collective-permute-done), channel_id=1, source_target_pairs={{0,1},{1,2},{2,3},{3,0},{4,5},{5,6},{6,7},{7,4},{8,9},{9,10},{10,1... | collective-permute-start | bytes 2359304 | tf_op jit(solution)/shard_map/ppermute | solution.py:13
  73.7 2.6 %copy-start = (pred[768,384]{0,1:T(8,128)(4,1)S(1)}, pred[768,384]{0,1:T(8,128)(4,1)}, u32[]{:S(2)}) copy-start(pred[768,384]{0,1:T(8,128)(4,1)} %get-tuple-element.42) | copy-start | bytes 884740
